TPU v7x, 256 devices: a whole 4x4x8 slice. The times are simulated.
256 devices in a mesh: dp: 8 (over x, core), fsdp: 8 (over z), mp: 4 (over y).
Axes of the slice: x: 4, y: 4, z: 8, core: 2. Of those that a mesh axis runs over, the one named last changes fastest.
Arguments:
- gradients: bfloat16 [64, 12, 2, 256, 1024], P(('dp', 'fsdp'), None, None, None, 'mp'), may hold values from -16 to 16
- master: float32 [12, 2, 256, 1024], P(None, None, ('dp', 'fsdp'), 'mp'), may hold values from -0.375 to 0.375
- teacher: float32 [12, 2, 256, 1024], P(None, None, ('dp', 'fsdp'), 'mp'), may hold values from -0.375 to 0.375
- first_moment: float32 [12, 2, 256, 1024], P(None, None, ('dp', 'fsdp'), 'mp'), may hold values from -2.2888184e-05 to 2.2888184e-05
- second_moment: float32 [12, 2, 256, 1024], P(None, None, ('dp', 'fsdp'), 'mp'), may hold values from 0 to 1, as said below
- layer_rates: float32 [12], replicated, may hold values from 0.02 to 0.2
Outputs:
- master_new: float32 [12, 2, 256, 1024], P(None, None, ('dp', 'fsdp'), 'mp')
- teacher_new: float32 [12, 2, 256, 1024], P(None, None, ('dp', 'fsdp'), 'mp')
- first_new: float32 [12, 2, 256, 1024], P(None, None, ('dp', 'fsdp'), 'mp')
- second_new: float32 [12, 2, 256, 1024], P(None, None, ('dp', 'fsdp'), 'mp')
- student_weights: bfloat16 [12, 2, 256, 1024], P(None, None, None, 'mp')
- teacher_weights: bfloat16 [12, 2, 256, 1024], P(None, None, None, 'mp')
Inputs may be any that keep to these rules, and one draw needn't show every extreme that they name: `second_moment`: every entry is positive.
All inputs are finite; a program needn't handle non-finite values.
Results may differ from a plain program's by a relative error of at most 0.0004.
Values may be sent and summed in bfloat16 or wider, within the bound.
No kernel may reach another device: no remote copies, remote signals or barrier semaphores. Data moves between devices by JAX's collectives and lax.ppermute only.
A program may use at most 64 MiB of HBM per device.

v0:
```python
import jax
import jax.numpy as jnp
from jax import lax
from jax.sharding import PartitionSpec as P

OWN = ("dp", "fsdp")
ALL = ("dp", "fsdp", "mp")
CLIP_NORM = 0.1
BETA_ONE = 0.9
BETA_TWO = 0.999
BIAS_ONE = 1.0 - 0.9**50 * 0.9**50
BIAS_TWO = 1.0 - 0.999**50 * 0.999**50
ADAM_EPS = 1e-08
DECAY = 0.05
EMA_KEEP = 0.95


def shards(gradients, master, teacher, first_moment, second_moment, layer_rates):
    own_grad = gradients[0].astype(jnp.float32)
    summed = lax.psum_scatter(own_grad, OWN, scatter_dimension=2, tiled=True)
    mean_grad = summed / 64.0
    norm_sq = lax.psum(jnp.sum(mean_grad * mean_grad), ALL)
    clip_factor = jnp.minimum(1.0, CLIP_NORM / (jnp.sqrt(norm_sq) + 1e-06))
    clipped = clip_factor * mean_grad
    first_new = BETA_ONE * first_moment + (1.0 - BETA_ONE) * clipped
    second_new = BETA_TWO * second_moment + (1.0 - BETA_TWO) * clipped * clipped
    direction = first_new / BIAS_ONE / (jnp.sqrt(second_new / BIAS_TWO) + ADAM_EPS) + DECAY * master
    layer_rate = layer_rates[:, None, None, None]
    master_new = master - layer_rate * direction
    teacher_new = EMA_KEEP * teacher + (1.0 - EMA_KEEP) * master_new
    student = lax.all_gather(master_new.astype(jnp.bfloat16), OWN, axis=2, tiled=True)
    teach = lax.all_gather(teacher_new.astype(jnp.bfloat16), OWN, axis=2, tiled=True)
    return (master_new, teacher_new, first_new, second_new, student, teach)


def solution(mesh):
    own = P(None, None, OWN, "mp")
    gathered = P(None, None, None, "mp")
    in_specs = (P(OWN, None, None, None, "mp"), own, own, own, own, P())
    out_specs = (own, own, own, own, gathered, gathered)
    return jax.shard_map(shards, mesh=mesh, in_specs=in_specs, out_specs=out_specs, check_vma=False)
```

profile of v0, /device:TPU:1, one launch (start us, length us, event | category | flops | bytes accessed | tf_op | source)
XLA Modules:
  0.0 413.0 jit_solution(480780248336302537)
XLA Ops:
  7.2 0.0 reduce-scatter.2.cloned.1.call-start
  7.2 7.0 %bitcast_convert_fusion = f32[12,2,256,256]{3,0,1,2:T(8,128)} fusion(bf16[1,12,2,256,256]{4,3,2,1,0:T(8,128)(2,1)} %param.6), kind=kLoop, calls=%fused_computation | loop fusion | flops 1572864 | bytes 9437184 | tf_op jit(solution)/shard_map/convert_element_type | solution.py:19
  14.2 0.0 copy-start
  14.2 0.0 copy-start.1
  14.2 0.0 copy-start.2
  14.2 0.0 copy-start.3
  14.2 0.0 copy-start.4
  14.2 0.0 reduce-scatter.2.cloned.1.call-update
  14.3 0.0 all-gather.3.cloned.1.call-start
  14.3 151.8 %reduce-scatter.2.cloned.1.call-done = f32[12,2,4,256]{3,0,1,2:T(8,128)} async-done(((f32[12,2,256,256]{3,0,1,2:T(8,128)}), f32[12,2,4,256]{3,0,1,2:T(8,128)}) %reduce-scatter.2.cloned.1.call-update) | async-done | bytes 98320 | tf_op jit(solution)/shard_map/reduce_scatter | solution.py:20
  166.1 1.5 multiply_reduce_fusion
  167.6 78.7 %psum.7 = f32[]{:T(128)} all-reduce(f32[]{:T(128)} %multiply_reduce_fusion), channel_id=1, replica_groups=mesh['dp'=8,'fsdp'=8,'mp'=4] {'dp','fsdp','mp'}, use_global_device_ids=true, to_apply=%region_2.0 | all-reduce | flops 1 | bytes 8 | tf_op jit(solution)/shard_map/psum | solution.py:22
  247.1 0.0 copy-done
  247.1 0.0 copy-done.1
  247.1 0.0 copy-done.2
  247.1 0.0 copy-done.3
  247.1 0.0 copy-done.4
  247.1 1.1 fusion.5
  248.3 0.7 copy.18
  248.9 0.0 all-gather.3.cloned.1.call-update
  249.0 0.0 all-gather.5.cloned.1.call-start
  249.0 0.7 copy.19
  249.7 0.0 all-gather.5.cloned.1.call-update
  249.7 0.7 copy.20
  250.4 0.7 copy.21
  251.1 0.7 copy.22
  251.8 0.7 copy.23
  252.5 71.5 %all-gather.3.cloned.1.call-done = bf16[12,2,256,256]{3,1,0,2:T(2,128)(2,1)} async-done(((bf16[12,2,4,256]{3,1,0,2:T(2,128)(2,1)}), bf16[12,2,256,256]{3,1,0,2:T(2,128)(2,1)}) %all-gather.3.cloned.1.call-update) | async-done | bytes 3145744 | tf_op jit(solution)/shard_map/all_gather | solution.py:31
  324.1 4.3 %copy.24 = bf16[12,2,256,256]{3,2,1,0:T(8,128)(2,1)} copy(bf16[12,2,256,256]{3,1,0,2:T(2,128)(2,1)} %all-gather.3.cloned.1.call-done) | data formatting | bytes 6291456
  328.4 73.9 %all-gather.5.cloned.1.call-done = bf16[12,2,256,256]{3,1,0,2:T(2,128)(2,1)} async-done(((bf16[12,2,4,256]{3,1,0,2:T(2,128)(2,1)}), bf16[12,2,256,256]{3,1,0,2:T(2,128)(2,1)}) %all-gather.5.cloned.1.call-update) | async-done | bytes 3145744 | tf_op jit(solution)/shard_map/all_gather | solution.py:32
  402.2 4.3 %copy.25 = bf16[12,2,256,256]{3,2,1,0:T(8,128)(2,1)} copy(bf16[12,2,256,256]{3,1,0,2:T(2,128)(2,1)} %all-gather.5.cloned.1.call-done) | data formatting | bytes 6291456
  (1 shorter events, 0.0 us)
Async XLA Ops:
  7.2 158.9 %reduce-scatter.2.cloned.1.call-start = ((), (), s32[]{:S(2)}) async-start(), calls=%async_computation.1 | async-start | bytes 8519680 | tf_op jit(solution)/shard_map/reduce_scatter | solution.py:20
  14.2 232.9 %copy-start = (f32[12,2,4,256]{3,2,1,0:T(4,128)S(1)}, f32[12,2,4,256]{3,2,1,0:T(4,128)}, u32[]{:S(2)}) copy-start(f32[12,2,4,256]{3,2,1,0:T(4,128)} %param.8) | copy-start | bytes 294916
  14.2 232.9 %copy-start.1 = (f32[12,2,4,256]{3,2,1,0:T(4,128)S(1)}, f32[12,2,4,256]{3,2,1,0:T(4,128)}, u32[]{:S(2)}) copy-start(f32[12,2,4,256]{3,2,1,0:T(4,128)} %param.7) | copy-start | bytes 294916
  14.2 232.9 %copy-start.2 = (f32[12,2,4,256]{3,2,1,0:T(4,128)S(1)}, f32[12,2,4,256]{3,2,1,0:T(4,128)}, u32[]{:S(2)}) copy-start(f32[12,2,4,256]{3,2,1,0:T(4,128)} %param.9) | copy-start | bytes 294916
  14.2 232.9 %copy-start.3 = (f32[12,2,4,256]{3,2,1,0:T(4,128)S(1)}, f32[12,2,4,256]{3,2,1,0:T(4,128)}, u32[]{:S(2)}) copy-start(f32[12,2,4,256]{3,2,1,0:T(4,128)} %param.10) | copy-start | bytes 294916
  14.2 232.9 %copy-start.4 = (f32[12]{0:T(128)S(1)}, f32[12]{0:T(128)}, u32[]{:S(2)}) copy-start(f32[12]{0:T(128)} %param.11) | copy-start | bytes 148
  14.3 309.8 %all-gather.3.cloned.1.call-start = ((), (), s32[]{:S(2)}) async-start(), calls=%async_computation.2 | async-start | bytes 3194880 | tf_op jit(solution)/shard_map/all_gather | solution.py:31
  249.0 153.3 %all-gather.5.cloned.1.call-start = ((), (), s32[]{:S(2)}) async-start(), calls=%async_computation.3 | async-start | bytes 3194880 | tf_op jit(solution)/shard_map/all_gather | solution.py:32
Sparse Core Ops, SparseCore 0:
  14.4 151.6 reduce-scatter.1
  249.1 74.9 all-gather.2
  326.8 75.3 all-gather.4
where the time goes:
time: 413 us
  waiting for transfers between devices  297 us (72%)
  blocking collectives  78.7 us (19%)
  between operations  14.5 us (4%)
  local copies, waits for them, and re-layouts  12.7 us (3%)
  other arithmetic  9.68 us (2%)
    reduce_scatter x1, waiting for transfers between devices, shards(): summed = lax.psum_scatter(own_grad, OWN, scatter_dimension=2, tiled=True)  152 us
    psum x1, blocking collectives, shards(): norm_sq = lax.psum(jnp.sum(mean_grad * mean_grad), ALL)  78.7 us
    all_gather x1, waiting for transfers between devices, shards(): lax.all_gather(teacher_new.astype(jnp.bfloat16), OWN, axis=2, tiled=True)  73.9 us
    all_gather x1, waiting for transfers between devices, shards(): lax.all_gather(master_new.astype(jnp.bfloat16), OWN, axis=2, tiled=True)  71.5 us
    unnamed x16, local copies, waits for them, and re-layouts  11.4 us
  transfers between devices with their start and end apart: 3, of which 3 were waited for; matrix products, arithmetic and copies ran while one was open for 2% of the time, Pallas kernels for 0%

commit v1 on v0

--- a/solution.py
+++ b/solution.py
@@ -28,7 +28,7 @@
     layer_rate = layer_rates[:, None, None, None]
     master_new = master - layer_rate * direction
     teacher_new = EMA_KEEP * teacher + (1.0 - EMA_KEEP) * master_new
-    student = lax.all_gather(master_new.astype(jnp.bfloat16), OWN, axis=2, tiled=True)
+    student = jnp.concatenate(lax.all_gather(master_new.astype(jnp.bfloat16), OWN), axis=2)
     teach = lax.all_gather(teacher_new.astype(jnp.bfloat16), OWN, axis=2, tiled=True)
     return (master_new, teacher_new, first_new, second_new, student, teach)
 

time: 413 us -> 413 us (level)
    reshape x0 -> x2, local copies, waits for them, and re-layouts: none -> 6.44 us  [shards(): jnp.concatenate(lax.all_gather(master_new.astype(jnp.bfloat16), OWN), axi...]
    unnamed x16 -> x15, local copies, waits for them, and re-layouts: 11.4 us -> 7.13 us
where the time goes in v1:
time: 413 us
  waiting for transfers between devices  295 us (71%)
  blocking collectives  78.7 us (19%)
  local copies, waits for them, and re-layouts  14.9 us (4%)
  between operations  14.6 us (4%)
  other arithmetic  9.68 us (2%)
    reduce_scatter x1, waiting for transfers between devices, shards(): summed = lax.psum_scatter(own_grad, OWN, scatter_dimension=2, tiled=True)  152 us
    psum x1, blocking collectives, shards(): norm_sq = lax.psum(jnp.sum(mean_grad * mean_grad), ALL)  78.7 us
    all_gather x1, waiting for transfers between devices, shards(): lax.all_gather(teacher_new.astype(jnp.bfloat16), OWN, axis=2, tiled=True)  71.7 us
    all_gather x1, waiting for transfers between devices, shards(): lax.all_gather(master_new.astype(jnp.bfloat16), OWN)  71.5 us
  transfers between devices with their start and end apart: 3, of which 3 were waited for; matrix products, arithmetic and copies ran while one was open for 2% of the time, Pallas kernels for 0%

profile of v1, /device:TPU:1, one launch (start us, length us, event | category | flops | bytes accessed | tf_op | source)
XLA Modules:
  0.0 413.0 jit_solution(5299644475290063555)
XLA Ops:
  7.2 0.0 reduce-scatter.2.cloned.1.call-start
  7.2 7.0 %bitcast_convert_fusion = f32[12,2,256,256]{3,0,1,2:T(8,128)} fusion(bf16[1,12,2,256,256]{4,3,2,1,0:T(8,128)(2,1)} %param.6), kind=kLoop, calls=%fused_computation | loop fusion | flops 1572864 | bytes 9437184 | tf_op jit(solution)/shard_map/convert_element_type | solution.py:19
  14.2 0.0 copy-start
  14.2 0.0 copy-start.1
  14.2 0.0 copy-start.2
  14.2 0.0 copy-start.3
  14.2 0.0 copy-start.4
  14.2 0.0 reduce-scatter.2.cloned.1.call-update
  14.3 0.0 all-gather.6.cloned.1.call-start
  14.3 151.8 %reduce-scatter.2.cloned.1.call-done = f32[12,2,4,256]{3,0,1,2:T(8,128)} async-done(((f32[12,2,256,256]{3,0,1,2:T(8,128)}), f32[12,2,4,256]{3,0,1,2:T(8,128)}) %reduce-scatter.2.cloned.1.call-update) | async-done | bytes 98320 | tf_op jit(solution)/shard_map/reduce_scatter | solution.py:20
  166.1 1.5 multiply_reduce_fusion
  167.6 78.7 %psum.7 = f32[]{:T(128)} all-reduce(f32[]{:T(128)} %multiply_reduce_fusion), channel_id=1, replica_groups=mesh['dp'=8,'fsdp'=8,'mp'=4] {'dp','fsdp','mp'}, use_global_device_ids=true, to_apply=%region_2.0 | all-reduce | flops 1 | bytes 8 | tf_op jit(solution)/shard_map/psum | solution.py:22
  247.1 0.0 copy-done
  247.1 0.0 copy-done.1
  247.1 0.0 copy-done.2
  247.1 0.0 copy-done.3
  247.1 0.0 copy-done.4
  247.1 1.1 fusion.5
  248.3 0.7 copy.19
  248.9 0.0 all-gather.6.cloned.1.call-update
  249.0 0.0 all-gather.4.cloned.1.call-start
  249.0 0.7 copy.21
  249.7 0.0 all-gather.4.cloned.1.call-update
  249.7 0.7 copy.22
  250.4 0.7 copy.23
  251.1 0.7 copy.24
  251.8 0.7 copy.25
  252.5 71.5 %all-gather.6.cloned.1.call-done = bf16[768,2,4,256]{3,2,1,0:T(4,128)(2,1)} async-done(((bf16[12,2,4,256]{3,2,1,0:T(4,128)(2,1)}), bf16[768,2,4,256]{3,2,1,0:T(4,128)(2,1)}) %all-gather.6.cloned.1.call-update) | async-done | bytes 3145744 | tf_op jit(solution)/shard_map/all_gather | solution.py:31
  324.1 3.5 copy.20
  327.6 2.9 reshape.22
  330.5 71.7 %all-gather.4.cloned.1.call-done = bf16[12,2,256,256]{3,1,0,2:T(2,128)(2,1)} async-done(((bf16[12,2,4,256]{3,1,0,2:T(2,128)(2,1)}), bf16[12,2,256,256]{3,1,0,2:T(2,128)(2,1)}) %all-gather.4.cloned.1.call-update) | async-done | bytes 3145744 | tf_op jit(solution)/shard_map/all_gather | solution.py:32
  402.2 4.3 %copy.26 = bf16[12,2,256,256]{3,2,1,0:T(8,128)(2,1)} copy(bf16[12,2,256,256]{3,1,0,2:T(2,128)(2,1)} %all-gather.4.cloned.1.call-done) | data formatting | bytes 6291456
  (1 shorter events, 0.0 us)
Async XLA Ops:
  7.2 158.9 %reduce-scatter.2.cloned.1.call-start = ((), (), s32[]{:S(2)}) async-start(), calls=%async_computation.1 | async-start | bytes 8519680 | tf_op jit(solution)/shard_map/reduce_scatter | solution.py:20
  14.2 232.9 %copy-start = (f32[12,2,4,256]{3,2,1,0:T(4,128)S(1)}, f32[12,2,4,256]{3,2,1,0:T(4,128)}, u32[]{:S(2)}) copy-start(f32[12,2,4,256]{3,2,1,0:T(4,128)} %param.8) | copy-start | bytes 294916
  14.2 232.9 %copy-start.1 = (f32[12,2,4,256]{3,2,1,0:T(4,128)S(1)}, f32[12,2,4,256]{3,2,1,0:T(4,128)}, u32[]{:S(2)}) copy-start(f32[12,2,4,256]{3,2,1,0:T(4,128)} %param.7) | copy-start | bytes 294916
  14.2 232.9 %copy-start.2 = (f32[12,2,4,256]{3,2,1,0:T(4,128)S(1)}, f32[12,2,4,256]{3,2,1,0:T(4,128)}, u32[]{:S(2)}) copy-start(f32[12,2,4,256]{3,2,1,0:T(4,128)} %param.9) | copy-start | bytes 294916
  14.2 232.9 %copy-start.3 = (f32[12,2,4,256]{3,2,1,0:T(4,128)S(1)}, f32[12,2,4,256]{3,2,1,0:T(4,128)}, u32[]{:S(2)}) copy-start(f32[12,2,4,256]{3,2,1,0:T(4,128)} %param.10) | copy-start | bytes 294916
  14.2 232.9 %copy-start.4 = (f32[12]{0:T(128)S(1)}, f32[12]{0:T(128)}, u32[]{:S(2)}) copy-start(f32[12]{0:T(128)} %param.11) | copy-start | bytes 148
  14.3 309.8 %all-gather.6.cloned.1.call-start = ((), (), s32[]{:S(2)}) async-start(), calls=%async_computation.3 | async-start | bytes 3194880 | tf_op jit(solution)/shard_map/all_gather | solution.py:31
  249.0 153.3 %all-gather.4.cloned.1.call-start = ((), (), s32[]{:S(2)}) async-start(), calls=%async_computation.2 | async-start | bytes 3194880 | tf_op jit(solution)/shard_map/all_gather | solution.py:32
Sparse Core Ops, SparseCore 0:
  14.4 151.6 reduce-scatter.1
  249.1 74.9 all-gather.5
  326.8 75.3 all-gather.3
